TPU v7x, 32 devices: a whole 2x2x4 slice. The times are simulated.
32 devices in a mesh: section: 2 (over x), dp: 16 (over z, y, core).
Axes of the slice: x: 2, y: 2, z: 4, core: 2. Of those that a mesh axis runs over, the one named last changes fastest.
Arguments:
- grads: bfloat16 [32, 524288], P(('section', 'dp')), parts along dimension 0, may hold values from -6 to 6
- master: float32 [32, 32768], P(('section', 'dp')), parts along dimension 0, may hold values from -30 to 30
- first_moment: float32 [32, 32768], P(('section', 'dp')), parts along dimension 0, may hold values from -0.6 to 0.6
- second_moment: float32 [32, 32768], P(('section', 'dp')), parts along dimension 0, may hold values from 0.005 to 0.05
- perm: int32 [32], P('section'), parts along dimension 0, may hold values from 0 to 15, each once
- bounds: int32 [34], P('section'), parts along dimension 0, may hold values from 0 to 524288, as said below
Outputs:
- new_weights: bfloat16 [1048576], P('section'), parts along dimension 0
- new_master: float32 [32, 32768], P(('section', 'dp')), parts along dimension 0
- new_first: float32 [32, 32768], P(('section', 'dp')), parts along dimension 0
- new_second: float32 [32, 32768], P(('section', 'dp')), parts along dimension 0
- step_taken: float32 [32, 32768], P(('section', 'dp')), parts along dimension 0
There are 2 independent parts, one for each index of `section`. A program takes and returns all parts, laid end to end along the dimension named above; each array names one. Nothing has to cross between parts.
Inputs may be any that keep to these rules, and one draw needn't show every extreme that they name: `perm`: each device index appears exactly once. `bounds`: strictly increasing multiples of 128, the first 0 and the last 524288.
All inputs are finite; a program needn't handle non-finite values.
Results may differ from a plain program's by a relative error of at most 0.0004.
Values may be sent and summed in bfloat16 or wider, within the bound.
No kernel may reach another device: no remote copies, remote signals or barrier semaphores. Data moves between devices by JAX's collectives and lax.ppermute only.
A program may use at most 128 MiB of HBM per device.

v0:
```python
import jax
import jax.numpy as jnp
from jax import lax
from jax.sharding import PartitionSpec as P

beta_first = 0.9
beta_second = 0.999
first_fix = 1.0 - 0.9**10
second_fix = 1.0 - 0.999**10
adam_eps = 1e-06
norm_eps = 1e-06
decay_rate = 0.01
learn_rate = 0.01


def per_device(grads, master, first_moment, second_moment, perm, bounds):
    replica_count = lax.axis_size("dp")
    shard_len = master.shape[1]
    own_block = perm[lax.axis_index("dp")]
    positions = own_block * shard_len + jnp.arange(shard_len, dtype=jnp.int32)
    member = (positions[None, :] >= bounds[:-1, None]) & (positions[None, :] < bounds[1:, None])
    onehot = member.astype(jnp.float32)
    weight_part = jnp.dot(onehot, master[0] * master[0], precision=lax.Precision.HIGHEST)
    summed = lax.psum(grads[0].astype(jnp.float32), "dp")
    own_grad = (
        lax.dynamic_slice_in_dim(summed, own_block * shard_len, shard_len)[None, :] / replica_count
    )
    new_first = beta_first * first_moment + (1.0 - beta_first) * own_grad
    new_second = beta_second * second_moment + (1.0 - beta_second) * own_grad * own_grad
    direction = (
        new_first / first_fix / (jnp.sqrt(new_second / second_fix) + adam_eps) + decay_rate * master
    )
    update_part = jnp.dot(onehot, direction[0] * direction[0], precision=lax.Precision.HIGHEST)
    weight_sq, update_sq = lax.psum((weight_part, update_part), "dp")
    trust_ratio = jnp.sqrt(weight_sq) / (jnp.sqrt(update_sq) + norm_eps)
    entry_ratio = jnp.dot(trust_ratio, onehot, precision=lax.Precision.HIGHEST)
    step_taken = entry_ratio[None, :] * direction
    new_master = master - learn_rate * step_taken
    gathered = lax.all_gather(new_master.astype(jnp.bfloat16), "dp", axis=0, tiled=True)
    inverse = jnp.argsort(perm)
    new_weights = jnp.take(gathered, inverse, axis=0).reshape(-1)
    return (new_weights, new_master, new_first, new_second, step_taken)


def solution(mesh):
    return jax.shard_map(
        per_device,
        mesh=mesh,
        in_specs=(
            P(("section", "dp"), None),
            P(("section", "dp"), None),
            P(("section", "dp"), None),
            P(("section", "dp"), None),
            P("section"),
            P("section"),
        ),
        out_specs=(
            P("section"),
            P(("section", "dp"), None),
            P(("section", "dp"), None),
            P(("section", "dp"), None),
            P(("section", "dp"), None),
        ),
        check_vma=False,
    )
```

profile of v0, /device:TPU:0, one launch (start us, length us, event | category | flops | bytes accessed | tf_op | source)
XLA Modules:
  0.0 200.4 jit_solution(13734129077697938728)
XLA Ops:
  7.2 0.0 all-reduce.3.cloned.1.call-start
  7.2 4.8 %convert_element_type.13 = f32[1,524288]{1,0:T(1,128)} convert(bf16[1,524288]{1,0:T(2,128)(2,1)} %param.6) | non-fusion elementwise | flops 524288 | bytes 3145728 | tf_op jit(solution)/shard_map/convert_element_type | solution.py:24
  12.0 0.0 copy-start.5
  12.0 0.0 copy-start.4
  12.0 0.0 copy-start
  12.0 0.0 copy-start.2
  12.0 0.0 copy-start.3
  12.0 0.0 all-reduce.3.cloned.1.call-update
  12.0 0.0 all-gather.3.cloned.1.call-start
  12.1 0.6 copy-done.5
  12.7 0.6 dynamic_slice.6
  13.9 0.0 copy-done.4
  13.9 0.1 fusion.17
  14.0 0.0 copy-done
  14.0 1.6 fusion.2
  15.6 97.5 %all-reduce.3.cloned.1.call-done = f32[524288]{0:T(1024)} async-done(((f32[524288]{0:T(1024)}), f32[524288]{0:T(1024)}) %all-reduce.3.cloned.1.call-update) | async-done | bytes 2097168 | tf_op jit(solution)/shard_map/psum | solution.py:24
  113.1 0.9 multiply_multiply_fusion
  114.0 0.0 copy-done.2
  114.0 0.0 copy-done.3
  114.0 1.4 multiply_add_fusion
  115.4 1.6 fusion.3
  117.1 30.4 %all-reduce = (f32[16]{0:T(128)S(1)}, f32[16]{0:T(128)S(1)}) all-reduce(f32[16]{0:T(128)S(1)} %fusion.3, f32[16]{0:T(128)S(1)} %fusion.2), channel_id=1, replica_groups=mesh['section'=2,'dp'=16] {'dp'}, use_global_device_ids=true, to_apply=%region_3.0 | all-reduce | flops 32 | bytes 256 | tf_op jit(solution)/shard_map/psum | solution.py:34
  147.5 0.9 convolution_multiply_fusion
  148.4 0.0 copy-start.1
  148.4 0.9 convert_bitcast_fusion
  149.4 0.0 all-gather.3.cloned.1.call-update
  149.4 1.3 sort.17
  150.7 37.5 %all-gather.3.cloned.1.call-done = bf16[16,1,32768]{2,1,0:T(2,128)(2,1)} async-done(((bf16[1,1,32768]{2,1,0:T(2,128)(2,1)}), bf16[16,1,32768]{2,1,0:T(2,128)(2,1)}) %all-gather.3.cloned.1.call-update) | async-done | bytes 1048592 | tf_op jit(solution)/shard_map/all_gather | solution.py:39
  188.2 2.7 %copy.14 = bf16[16,1,32768]{2,0,1:T(8,128)(2,1)S(1)} copy(bf16[16,1,32768]{2,1,0:T(2,128)(2,1)} %all-gather.3.cloned.1.call-done) | data formatting | bytes 2097152
  191.0 1.2 gather_fusion
  192.2 0.0 copy-done.1
  192.2 0.2 select_bitcast_fusion
  192.4 1.2 copy.12
  (5 shorter events, 0.0 us)
Async XLA Ops:
  7.2 105.9 %all-reduce.3.cloned.1.call-start = ((), (), s32[]{:S(2)}) async-start(), calls=%async_computation | async-start | bytes 4194304 | tf_op jit(solution)/shard_map/psum | solution.py:24
  12.0 0.7 copy-start.5
  12.0 1.9 copy-start.4
  12.0 2.0 copy-start
  12.0 102.0 %copy-start.2 = (f32[1,32768]{1,0:T(1,128)S(1)}, f32[1,32768]{1,0:T(1,128)}, u32[]{:S(2)}) copy-start(f32[1,32768]{1,0:T(1,128)} %param.8) | copy-start | bytes 393220
  12.0 102.0 %copy-start.3 = (f32[1,32768]{1,0:T(1,128)S(1)}, f32[1,32768]{1,0:T(1,128)}, u32[]{:S(2)}) copy-start(f32[1,32768]{1,0:T(1,128)} %param.9) | copy-start | bytes 393220
  12.0 176.2 %all-gather.3.cloned.1.call-start = ((), (), s32[]{:S(2)}) async-start(), calls=%async_computation.1 | async-start | bytes 2228224 | tf_op jit(solution)/shard_map/all_gather | solution.py:39
  148.4 43.8 %copy-start.1 = (f32[1,32768]{1,0:T(1,128)}, f32[1,32768]{1,0:T(1,128)S(1)}, u32[]{:S(2)}) copy-start(f32[1,32768]{1,0:T(1,128)S(1)} %convolution_multiply_fusion) | copy-start | bytes 393220
Sparse Core Ops, SparseCore 0:
  12.2 100.8 all-reduce.2
  149.5 38.6 all-gather.2
where the time goes:
time: 201 us; the launch traced here: 200 us
  waiting for transfers between devices  135 us (67%)
  blocking collectives  30.4 us (15%)
  between operations  14.8 us (7%)
  other arithmetic  9.55 us (5%)
  local copies, waits for them, and re-layouts  6.37 us (3%)
  matrix products  4.16 us (2%)
    psum x1, waiting for transfers between devices, per_device(): summed = lax.psum(grads[0].astype(jnp.float32), 'dp')  97.5 us
    all_gather x1, waiting for transfers between devices, per_device(): lax.all_gather(new_master.astype(jnp.bfloat16), 'dp', axis=0, tiled=True)  37.5 us
    psum x1, blocking collectives, per_device(): weight_sq, update_sq = lax.psum((weight_part, update_part), 'dp')  30.4 us
    convert_element_type x1, other arithmetic, per_device(): summed = lax.psum(grads[0].astype(jnp.float32), 'dp')  4.79 us
    unnamed x14, local copies, waits for them, and re-layouts  4.48 us
  transfers between devices with their start and end apart: 2, of which 2 were waited for; matrix products, arithmetic and copies ran while one was open for 2% of the time, Pallas kernels for 0%

commit v1 on v0

--- a/solution.py
+++ b/solution.py
@@ -21,7 +21,8 @@
     member = (positions[None, :] >= bounds[:-1, None]) & (positions[None, :] < bounds[1:, None])
     onehot = member.astype(jnp.float32)
     weight_part = jnp.dot(onehot, master[0] * master[0], precision=lax.Precision.HIGHEST)
-    summed = lax.psum(grads[0].astype(jnp.float32), "dp")
+    piece_in = grads[0].astype(jnp.float32)
+    summed = lax.all_gather(piece_in, "dp").sum(axis=0)
     own_grad = (
         lax.dynamic_slice_in_dim(summed, own_block * shard_len, shard_len)[None, :] / replica_count
     )

time: 201 us -> 296 us (1.47)
  waiting for transfers between devices: 135 us -> 205 us
  other arithmetic: 9.55 us -> 33.2 us
    all_gather x0 -> x1, waiting for transfers between devices: none -> 167 us  [per_device(): summed = lax.all_gather(piece_in, 'dp').sum(axis=0)]
    psum x1 -> x0, waiting for transfers between devices: 97.5 us -> none  [per_device(): summed = lax.psum(grads[0].astype(jnp.float32), 'dp')]
    reduce_sum x0 -> x1, other arithmetic: none -> 24.5 us  [per_device(): summed = lax.all_gather(piece_in, 'dp').sum(axis=0)]
    unnamed x2 -> x3, other arithmetic: 1.1 us -> 5.92 us
    convert_element_type x1 -> x0, other arithmetic: 4.79 us -> none  [per_device(): summed = lax.psum(grads[0].astype(jnp.float32), 'dp')]
  transfers between devices with their start and end apart: 2 -> 2, of which waited for: 2 -> 2; matrix products, arithmetic and copies ran while one was open for 2% -> 1% of each run, Pallas kernels for 0% -> 0%
where the time goes in v1:
time: 296 us
  waiting for transfers between devices  205 us (69%)
  other arithmetic  33.2 us (11%)
  blocking collectives  32.6 us (11%)
  between operations  14.8 us (5%)
  local copies, waits for them, and re-layouts  6.41 us (2%)
  matrix products  4.16 us (1%)
    all_gather x1, waiting for transfers between devices, per_device(): summed = lax.all_gather(piece_in, 'dp').sum(axis=0)  167 us
    all_gather x1, waiting for transfers between devices, per_device(): lax.all_gather(new_master.astype(jnp.bfloat16), 'dp', axis=0, tiled=True)  37.5 us
    psum x1, blocking collectives, per_device(): weight_sq, update_sq = lax.psum((weight_part, update_part), 'dp')  32.6 us
    reduce_sum x1, other arithmetic, per_device(): summed = lax.all_gather(piece_in, 'dp').sum(axis=0)  24.5 us
    unnamed x3, other arithmetic  5.92 us
  transfers between devices with their start and end apart: 2, of which 2 were waited for; matrix products, arithmetic and copies ran while one was open for 1% of the time, Pallas kernels for 0%

profile of v1, /device:TPU:0, one launch (start us, length us, event | category | flops | bytes accessed | tf_op | source)
XLA Modules:
  0.0 296.2 jit_solution(17132078166889588620)
XLA Ops:
  7.2 0.0 all-gather.5.cloned.1.call-start
  7.2 4.8 %bitcast_convert_fusion = f32[1,1,524288]{2,1,0:T(1,128)} fusion(bf16[1,524288]{1,0:T(2,128)(2,1)} %param.6), kind=kLoop, calls=%fused_computation.2 | loop fusion | flops 524288 | bytes 3145728
  12.0 0.0 copy-start.5
  12.0 0.0 copy-start.4
  12.0 0.0 copy-start
  12.0 0.0 all-gather.5.cloned.1.call-update
  12.0 0.0 all-gather.7.cloned.1.call-start
  12.1 0.6 copy-done.5
  12.7 0.6 dynamic_slice.6
  13.9 0.0 copy-done.4
  13.9 0.1 fusion.17
  14.0 0.0 copy-done
  14.0 1.6 fusion.2
  15.6 0.0 copy-start.2
  15.7 0.0 copy-start.3
  15.7 167.3 %all-gather.5.cloned.1.call-done = f32[16,1,524288]{2,1,0:T(1,128)} async-done(((f32[1,1,524288]{2,1,0:T(1,128)}), f32[16,1,524288]{2,1,0:T(1,128)}) %all-gather.5.cloned.1.call-update) | async-done | bytes 33554448 | tf_op jit(solution)/shard_map/all_gather | solution.py:25
  183.0 24.5 %reduce_sum.9 = f32[524288]{0:T(1024)S(1)} reduce(f32[16,1,524288]{2,1,0:T(1,128)} %all-gather.5.cloned.1.call-done, f32[]{:T(128)} %constant.13.clone.1), dimensions={0,1}, to_apply=%region_2.0 | reduce | flops 7864320 | bytes 35651588 | tf_op jit(solution)/shard_map/reduce_sum | solution.py:25
  207.6 0.0 copy-done.2
  207.6 0.0 copy-done.3
  207.6 1.4 multiply_add_fusion
  209.0 1.6 fusion.3
  210.6 32.6 %all-reduce = (f32[16]{0:T(128)S(1)}, f32[16]{0:T(128)S(1)}) all-reduce(f32[16]{0:T(128)S(1)} %fusion.3, f32[16]{0:T(128)S(1)} %fusion.2), channel_id=1, replica_groups=mesh['section'=2,'dp'=16] {'dp'}, use_global_device_ids=true, to_apply=%region_3.0 | all-reduce | flops 32 | bytes 256 | tf_op jit(solution)/shard_map/psum | solution.py:35
  243.2 0.9 convolution_multiply_fusion
  244.2 0.0 copy-start.1
  244.2 1.0 convert_bitcast_fusion
  245.1 0.0 all-gather.7.cloned.1.call-update
  245.2 1.3 sort.17
  246.5 37.5 %all-gather.7.cloned.1.call-done = bf16[16,1,32768]{2,1,0:T(2,128)(2,1)} async-done(((bf16[1,1,32768]{2,1,0:T(2,128)(2,1)}), bf16[16,1,32768]{2,1,0:T(2,128)(2,1)}) %all-gather.7.cloned.1.call-update) | async-done | bytes 1048592 | tf_op jit(solution)/shard_map/all_gather | solution.py:40
  284.0 2.7 copy.14
  286.7 1.2 gather_fusion
  288.0 0.0 copy-done.1
  288.0 0.2 select_bitcast_fusion
  288.2 1.2 copy.12
  (6 shorter events, 0.1 us)
Async XLA Ops:
  7.2 175.8 %all-gather.5.cloned.1.call-start = ((), (), s32[]{:S(2)}) async-start(), calls=%async_computation | async-start | bytes 35651584 | tf_op jit(solution)/shard_map/all_gather | solution.py:25
  12.0 0.7 copy-start.5
  12.0 1.9 copy-start.4
  12.0 2.0 copy-start
  12.0 271.9 %all-gather.7.cloned.1.call-start = ((), (), s32[]{:S(2)}) async-start(), calls=%async_computation.1 | async-start | bytes 2228224 | tf_op jit(solution)/shard_map/all_gather | solution.py:40
  15.6 191.9 %copy-start.2 = (f32[1,32768]{1,0:T(1,128)S(1)}, f32[1,32768]{1,0:T(1,128)}, u32[]{:S(2)}) copy-start(f32[1,32768]{1,0:T(1,128)} %param.8) | copy-start | bytes 393220
  15.7 191.9 %copy-start.3 = (f32[1,32768]{1,0:T(1,128)S(1)}, f32[1,32768]{1,0:T(1,128)}, u32[]{:S(2)}) copy-start(f32[1,32768]{1,0:T(1,128)} %param.9) | copy-start | bytes 393220
  244.2 43.8 %copy-start.1 = (f32[1,32768]{1,0:T(1,128)}, f32[1,32768]{1,0:T(1,128)S(1)}, u32[]{:S(2)}) copy-start(f32[1,32768]{1,0:T(1,128)S(1)} %convolution_multiply_fusion) | copy-start | bytes 393220
Sparse Core Ops, SparseCore 0:
  12.2 170.7 all-gather.4
  245.3 38.6 all-gather.6
